TPU v7x, 32 devices: a whole 2x2x4 slice. The times are simulated.
32 devices in a mesh: freq: 8 (over y, x, core), base: 4 (over z).
Axes of the slice: x: 2, y: 2, z: 4, core: 2. Of those that a mesh axis runs over, the one named last changes fastest.
Arguments:
- visibility: float32 [2, 16, 2048], P(None, 'freq', 'base'), may hold values from -6 to 6
- tile_of: int32 [16, 2048, 1], P('freq', 'base'), may hold values from 0 to 3; in each aligned block of 512 rows (0 to 511, 512 to 1023, ..., all dimensions but the last counted through in order) at most 256 rows name the same one
- u_within: int32 [16, 2048], P('freq', 'base'), may hold values from 0 to 255
- v_cell: int32 [16, 2048], P('freq', 'base'), may hold values from 0 to 1016
- kernel_index: int32 [2, 16, 2048], P(None, 'freq', 'base'), may hold values from 0 to 127
- kernel: float32 [128, 8], replicated, may hold values from 0.1 to 1
- live_count: int32 [16, 4], P('freq', 'base'), may hold values from 64 to 512, as said below
- bin_map: int32 [1024, 1024], P('base'), may hold values from 0 to 511, as said below
Outputs:
- power_map: float32 [1024, 1024], P('freq', 'base')
- spectrum: float32 [512], replicated
Inputs may be any that keep to these rules, and one draw needn't show every extreme that they name: `tile_of`: among the visibilities of one channel on one device, at most 256 name the same tile, and in some device's visibilities a tile is named by exactly 256. `live_count`: the first device along base holds 512 used slots in every channel; the used slots of a device are its first ones. `bin_map`: every bin number occurs.
All inputs are finite; a program needn't handle non-finite values.
Results may differ from a plain program's by a relative error of at most 0.0003.
Values sent between devices are 32-bit elements; how exact they have to be, the bound alone decides.
A program may use at most 128 MiB of HBM per device.

v0:
```python
import functools
import math

import jax
import jax.numpy as jnp
import numpy as np
from jax import lax
from jax.experimental import pallas as pl
from jax.experimental.pallas import tpu as pltpu
from jax.sharding import PartitionSpec as P

NBINS = 512
BIN_LOW = 32
KW = 8
FINE = 32
SPREAD = FINE + KW
RADIX = 4
GROUP = 16


def halves_of(x):
    high = x.astype(jnp.bfloat16)
    low = (x - high.astype(jnp.float32)).astype(jnp.bfloat16)
    return high, low


def numpy_halves(x):
    x = np.asarray(x, np.float32)
    high = x.astype(jnp.bfloat16)
    low = (x - high.astype(np.float32)).astype(jnp.bfloat16)
    return high, low


def turn(product, grid):
    angle = (product % grid) * (2.0 * math.pi / grid)
    return np.cos(angle), np.sin(angle)


@functools.lru_cache(None)
def tables(grid, blocks):
    width = grid // blocks
    l = np.arange(grid)
    c, s = turn(np.arange(SPREAD)[:, None] * l[None, :], grid)
    c, s = (x.reshape(SPREAD, blocks, width) for x in (c, s))
    fine = np.concatenate(
        [np.concatenate([c, -s], axis=2), np.concatenate([s, c], axis=2)], axis=0
    ).transpose(1, 0, 2)
    fh, fl = numpy_halves(fine)
    pad = np.zeros((blocks, 256 - 6 * SPREAD, 2 * width), fh.dtype)
    fine = np.concatenate([fh, fl, fh, pad], axis=1)
    coarse_count = grid // FINE
    c, s = turn(np.arange(coarse_count)[:, None] * FINE * l[None, :], grid)
    c, s = (x.reshape(coarse_count, blocks, width) for x in (c, s))
    ch, cl = numpy_halves(np.concatenate([c, -s], axis=2).transpose(1, 0, 2))
    coarse = np.concatenate([ch, cl], axis=1)
    slab = grid // RADIX
    u = RADIX * np.arange(slab)[None, None, :] + np.arange(RADIX)[:, None, None]
    c, s = turn(np.arange(slab)[None, :, None] * u, grid)
    dh, dl = numpy_halves(np.concatenate([c, s], axis=1))
    return fine, coarse, dh, dl


def dot(a, b):
    return jnp.dot(a, b, preferred_element_type=jnp.float32)


def dot_slots(a, b):
    return lax.dot_general(a, b, (((0,), (0,)), ((), ())), preferred_element_type=jnp.float32)


def image_kernel(
    grid, scale, f_ref, fine_ref, coarse_ref, dh_ref, dl_ref, out_ref, q_ref, rh_ref, rl_ref,
    wh_ref, wl_ref, zh_ref, zl_ref, h_ref, y_ref
):
    channel, chunk = pl.program_id(0), pl.program_id(1)
    chunks = pl.num_programs(1)
    slots = f_ref.shape[2]
    width = out_ref.shape[1]
    slab = grid // RADIX
    period = RADIX * GROUP
    re, im = f_ref[0, 0:1, :], f_ref[0, 1:2, :]
    u = f_ref[0, 2:3, :].astype(jnp.int32)
    v = f_ref[0, 3:4, :].astype(jnp.int32)

    for first in range(RADIX):
        residue = RADIX * lax.broadcasted_iota(jnp.int32, (GROUP, slots), 0) + first
        tap = (residue - u) & (period - 1)
        group = (u + tap - residue) // period
        r = jnp.zeros((GROUP, slots), jnp.float32)
        for t in range(KW):
            r = jnp.where(tap == t, f_ref[0, 4 + t:5 + t, :], r)
        rh, rl = halves_of(r)
        q_ref[first] = group.astype(jnp.float32).astype(jnp.bfloat16)
        rh_ref[first] = rh
        rl_ref[first] = rl

    piece = min(512, slots)
    for start in range(0, slots, piece):
        at = slice(start, start + piece)
        vp = v[:, at]
        offset = lax.broadcasted_iota(jnp.int32, (SPREAD, piece), 0) - (vp & (FINE - 1))
        spread = jnp.zeros((SPREAD, piece), jnp.float32)
        for t in range(KW):
            spread = jnp.where(offset == t, f_ref[0, 4 + KW + t:5 + KW + t, at], spread)
        both = jnp.concatenate([spread * re[:, at], spread * im[:, at]], axis=0)
        bh, bl = halves_of(both)
        pad = jnp.zeros((256 - 6 * SPREAD, piece), jnp.bfloat16)
        zb = dot_slots(jnp.concatenate([bh, bh, bl, pad], axis=0), fine_ref[...])
        count = coarse_ref.shape[0]
        pick = lax.broadcasted_iota(jnp.int32, (count, piece), 0) & (count // 2 - 1)
        onehot = jnp.where(pick == vp // FINE, 1.0, 0.0).astype(jnp.bfloat16)
        e = dot_slots(onehot, coarse_ref[...])
        zr, zi = zb[:, :width], zb[:, width:]
        er, ei = e[:, :width], e[:, width:]
        z = jnp.concatenate([zr * er - zi * ei, zr * ei + zi * er], axis=1)
        zh, zl = halves_of(z)
        zh_ref[at, :] = zh
        zl_ref[at, :] = zl

    def slab_step(first, carry):
        q, rh, rl = q_ref[first], rh_ref[first], rl_ref[first]
        zero = jnp.zeros_like(rh)
        for g in range(slab // GROUP):
            hit = q == jnp.bfloat16(g)
            wh_ref[g * GROUP:(g + 1) * GROUP, :] = jnp.where(hit, rh, zero)
            wl_ref[g * GROUP:(g + 1) * GROUP, :] = jnp.where(hit, rl, zero)
        zh = zh_ref[...]
        wh = wh_ref[...]
        rows = dot(wh, zh) + dot(wh, zl_ref[...]) + dot(wl_ref[...], zh)

        @pl.when(chunk == 0)
        def _():
            h_ref[first] = rows

        @pl.when(chunk > 0)
        def _():
            h_ref[first] += rows

        return carry

    lax.fori_loop(0, RADIX, slab_step, 0)

    @pl.when((channel == 0) & (chunk == 0))
    def _():
        out_ref[...] = jnp.zeros_like(out_ref)

    @pl.when(chunk == chunks - 1)
    def _():
        def transform_step(first, carry):
            hh, hl = halves_of(h_ref[first])
            dh = dh_ref[first]
            y_ref[first] = dot(dh, hh) + dot(dh, hl) + dot(dl_ref[first], hh)
            return carry

        lax.fori_loop(0, RADIX, transform_step, 0)

        def combine(block, carry):
            rows = 32
            top = pl.multiple_of(block * rows, rows)
            low = pl.multiple_of(slab + block * rows, rows)
            yr, yi = [], []
            for first in range(RADIX):
                cy = y_ref[first, pl.ds(top, rows), :]
                sy = y_ref[first, pl.ds(low, rows), :]
                yr.append(cy[:, :width] + sy[:, width:])
                yi.append(cy[:, width:] - sy[:, :width])
            ar, ai = yr[0] + yr[2], yi[0] + yi[2]
            br, bi = yr[0] - yr[2], yi[0] - yi[2]
            cr, ci = yr[1] + yr[3], yi[1] + yi[3]
            dr, di = yr[1] - yr[3], yi[1] - yi[3]
            parts = [
                (ar + cr, ai + ci), (br + di, bi - dr), (ar - cr, ai - ci), (br - di, bi + dr)
            ]
            for k, (xr, xi) in enumerate(parts):
                at = pl.ds(pl.multiple_of(k * slab + block * rows, rows), rows)
                out_ref[at, :] += (xr * xr + xi * xi) * scale
            return carry

        lax.fori_loop(0, slab // 32, combine, 0)


def image_power(fields, fine, coarse, dh, dl, grid, scale):
    channels, field_count, total = fields.shape
    width = fine.shape[1] // 2
    chunk = min(2048, total)
    slab = grid // RADIX
    bf16, f32 = jnp.bfloat16, jnp.float32
    full = lambda x: pl.BlockSpec(x.shape, lambda c, n: (0,) * x.ndim)
    return pl.pallas_call(
        functools.partial(image_kernel, grid, scale),
        grid=(channels, total // chunk),
        out_shape=jax.ShapeDtypeStruct((grid, width), f32),
        in_specs=[
            pl.BlockSpec((1, field_count, chunk), lambda c, n: (c, 0, n)),
            full(fine), full(coarse), full(dh), full(dl),
        ],
        out_specs=pl.BlockSpec((grid, width), lambda c, n: (0, 0)),
        scratch_shapes=[
            pltpu.VMEM((RADIX, GROUP, chunk), bf16),
            pltpu.VMEM((RADIX, GROUP, chunk), bf16),
            pltpu.VMEM((RADIX, GROUP, chunk), bf16),
            pltpu.VMEM((slab, chunk), bf16),
            pltpu.VMEM((slab, chunk), bf16),
            pltpu.VMEM((chunk, 2 * width), bf16),
            pltpu.VMEM((chunk, 2 * width), bf16),
            pltpu.VMEM((RADIX, slab, 2 * width), f32),
            pltpu.VMEM((RADIX, 2 * slab, 2 * width), f32),
        ],
        compiler_params=pltpu.CompilerParams(
            vmem_limit_bytes=60 * 2**20, dimension_semantics=("arbitrary", "arbitrary")
        ),
    )(fields, fine, coarse, dh, dl)


def histogram_kernel(power_ref, bins_ref, out_ref, a_ref, b_ref):
    rows, columns = power_ref.shape
    high_count = NBINS // BIN_LOW
    bins = bins_ref[...].T
    for k in range(rows):
        at = slice(k * columns, (k + 1) * columns)
        value = power_ref[k:k + 1, :]
        bin_id = bins[k:k + 1, :]
        hit = lax.broadcasted_iota(jnp.int32, (high_count, columns), 0) == bin_id // BIN_LOW
        high = value.astype(jnp.bfloat16).astype(jnp.float32)
        low = value - high
        a_ref[0:high_count, at] = jnp.where(hit, high, 0.0).astype(jnp.bfloat16)
        a_ref[high_count:2 * high_count, at] = jnp.where(hit, low, 0.0).astype(jnp.bfloat16)
        a_ref[2 * high_count:, at] = jnp.where(hit, 1.0, 0.0).astype(jnp.bfloat16)
        hit = lax.broadcasted_iota(jnp.int32, (BIN_LOW, columns), 0) == bin_id % BIN_LOW
        b_ref[:, at] = jnp.where(hit, 1.0, 0.0).astype(jnp.bfloat16)
    sums = lax.dot_general(
        a_ref[...], b_ref[...], (((1,), (1,)), ((), ())), preferred_element_type=jnp.float32
    )
    out_ref[0] = sums[:high_count] + sums[high_count:2 * high_count]
    out_ref[1] = sums[2 * high_count:]


def histogram(power, bins):
    high_count = NBINS // BIN_LOW
    return pl.pallas_call(
        histogram_kernel,
        out_shape=jax.ShapeDtypeStruct((2, high_count, BIN_LOW), jnp.float32),
        scratch_shapes=[
            pltpu.VMEM((3 * high_count, power.size), jnp.bfloat16),
            pltpu.VMEM((BIN_LOW, power.size), jnp.bfloat16),
        ],
    )(power, bins)


def look_up_taps(kernel_index, kernel):
    rows = kernel.shape[0]
    onehot = (kernel_index[:, :, None, :] == jnp.arange(rows, dtype=jnp.int32)[:, None]).astype(
        jnp.float32
    )
    return jnp.einsum("acon,ot->actn", onehot, kernel, precision=lax.Precision.HIGHEST)


def per_device(visibility, tile_of, u_within, v_cell, kernel_index, kernel, live_count, bin_map):
    base_count = lax.axis_size("base")
    freq_count = lax.axis_size("freq")
    grid = bin_map.shape[1]
    tile_rows = grid // base_count
    channels_here, slots = u_within.shape
    fine, coarse, dh, dl = tables(grid, base_count)
    here = lax.axis_index("base")
    fine = lax.dynamic_index_in_dim(jnp.asarray(fine), here, 0, keepdims=False)
    coarse = lax.dynamic_index_in_dim(jnp.asarray(coarse), here, 0, keepdims=False)

    is_live = jnp.arange(slots, dtype=jnp.int32)[None, :] < live_count
    vis = jnp.where(is_live[None], visibility, 0.0)
    u_cell = jnp.minimum(tile_of[:, :, 0] * tile_rows + u_within, grid - KW)
    taps = look_up_taps(kernel_index, kernel)
    fields = jnp.concatenate(
        [
            vis.transpose(1, 0, 2),
            u_cell[:, None].astype(jnp.float32),
            v_cell[:, None].astype(jnp.float32),
            taps[0],
            taps[1],
            jnp.zeros((channels_here, 4, slots), jnp.float32),
        ],
        axis=1,
    )
    fields = lax.all_gather(fields, "base", axis=2, tiled=True)
    scale = 1.0 / (channels_here * freq_count * slots * base_count)
    power_part = image_power(fields, fine, coarse, jnp.asarray(dh), jnp.asarray(dl), grid, scale)
    share_rows = grid // freq_count
    power_share = lax.psum_scatter(power_part, "freq", scatter_dimension=0, tiled=True)
    bins_share = lax.dynamic_slice_in_dim(
        bin_map, lax.axis_index("freq") * share_rows, share_rows, 1
    )
    sums = lax.psum(histogram(power_share, bins_share), ("freq", "base"))
    return (power_share, (sums[0] / sums[1]).reshape(NBINS))


def solution(mesh):
    in_specs = (
        P(None, "freq", "base"),
        P("freq", "base", None),
        P("freq", "base"),
        P("freq", "base"),
        P(None, "freq", "base"),
        P(),
        P("freq", "base"),
        P("base", None),
    )
    out_specs = (P("freq", "base"), P())
    return jax.shard_map(
        per_device, mesh=mesh, in_specs=in_specs, out_specs=out_specs, check_vma=False
    )
```

profile of v0, /device:TPU:0, one launch (start us, length us, event | category | flops | bytes accessed | tf_op | source)
XLA Modules:
  0.0 146.9 jit_solution(1029445984085662931)
XLA Ops:
  7.2 0.0 copy-start
  7.2 0.0 reduce-scatter.2.cloned.1.call-start
  7.2 1.8 %dynamic-slice_bitcast_fusion.fine_ref = bf16[256,512]{1,0:T(8,128)(2,1)} fusion(bf16[4,256,512]{2,1,0:T(8,128)(2,1)} %constant.39.clone, s32[]{:T(128)S(6)} %select_n.14), kind=kLoop, calls=%fused_computation.3 | loop fusion | bytes 524292 | tf_op jit(solution)/shard_map/jit(dynamic_index_in_dim)/squeeze | solution.py:266
  9.0 0.0 copy-start.6
  9.0 0.0 copy-start.7
  9.0 1.5 %dynamic-slice_bitcast_fusion.1.coarse_ref = bf16[64,512]{1,0:T(8,128)(2,1)} fusion(bf16[4,64,512]{2,1,0:T(8,128)(2,1)} %constant.40.clone, s32[]{:T(128)S(6)} %select_n.14), kind=kLoop, calls=%fused_computation.4 | loop fusion | bytes 131076 | tf_op jit(solution)/shard_map/jit(dynamic_index_in_dim)/squeeze | solution.py:267
  10.5 0.0 copy-done.6
  10.5 0.0 copy-done.7
  10.5 0.4 convolution_bitcast_fusion
  10.9 0.0 copy-start.5
  10.9 0.0 copy-start.3
  11.0 0.0 copy-start.2
  11.0 0.6 copy-done.5
  11.6 0.1 iota_compare_fusion.2
  11.7 0.0 copy-done.3
  11.7 0.0 copy-done.2
  11.7 0.0 copy-start.4
  11.7 0.7 copy-done.4
  12.4 0.0 copy-start.1
  12.4 0.7 copy-done.1
  13.1 0.3 concatenate.3
  13.4 16.8 %all_gather.3.f_ref = f32[2,24,2048]{2,1,0:T(8,128)} all-gather(f32[2,24,512]{2,1,0:T(8,128)S(1)} %concatenate.3), channel_id=1, replica_groups=mesh['freq'=8,'base'=4] {'base'}, dimensions={2}, use_global_device_ids=true | all-gather | bytes 491520 | tf_op jit(solution)/shard_map/all_gather | solution.py:284
  30.1 28.9 %shard_map.131 = f32[1024,256]{1,0:T(8,128)} custom-call(f32[2,24,2048]{2,1,0:T(8,128)} %all_gather.3.f_ref, bf16[256,512]{1,0:T(8,128)(2,1)} %dynamic-slice_bitcast_fusion.fine_ref, bf16[64,512]{1,0:T(8,128)(2,1)} %dynamic-slice_bitcast_fusion.1.coarse_ref, bf16[4,512,256]{2,1,0:T(8,128)(2,1)} %constant.41.clone.dh_ref, ...), custom_call_target="tpu_custom_call" | custom-call | tf_op jit(solution)/shard_map/pallas_call | solution.py:189
  59.1 0.0 reduce-scatter.2.cloned.1.call-update
  59.1 0.0 copy-done
  59.1 0.7 constant_dynamic-slice_fusion.bins_ref
  59.8 37.3 %reduce-scatter.2.cloned.1.call-done.power_ref = f32[128,256]{1,0:T(8,128)} async-done(((f32[1024,256]{1,0:T(8,128)}), f32[128,256]{1,0:T(8,128)}) %reduce-scatter.2.cloned.1.call-update) | async-done | bytes 131088 | tf_op jit(solution)/shard_map/reduce_scatter | solution.py:288
  97.0 2.8 %shard_map.132 = f32[2,16,32]{2,1,0:T(8,128)} custom-call(f32[128,256]{1,0:T(8,128)} %reduce-scatter.2.cloned.1.call-done.power_ref, s32[256,128]{1,0:T(8,128)} %constant_dynamic-slice_fusion.bins_ref), custom_call_target="tpu_custom_call" | custom-call | tf_op jit(solution)/shard_map/pallas_call | solution.py:240
  99.9 39.5 %psum.7 = f32[2,16,32]{2,1,0:T(8,128)S(1)} all-reduce(f32[2,16,32]{2,1,0:T(8,128)} %shard_map.132), channel_id=1, replica_groups=mesh['freq'=8,'base'=4] {'freq','base'}, use_global_device_ids=true, to_apply=%region_1.2 | all-reduce | flops 1024 | bytes 8192 | tf_op jit(solution)/shard_map/psum | solution.py:292
  139.4 0.7 div.8
  (8 shorter events, 0.0 us)
Async XLA Ops:
  7.2 51.9 %copy-start = (s32[256,1024]{1,0:T(8,128)S(1)}, s32[256,1024]{1,0:T(8,128)}, u32[]{:S(2)}) copy-start(s32[256,1024]{1,0:T(8,128)} %param.19) | copy-start | bytes 3145732
  7.2 89.9 %reduce-scatter.2.cloned.1.call-start = ((), (), s32[]{:S(2)}) async-start(), calls=%async_computation.1 | async-start | bytes 1179648 | tf_op jit(solution)/shard_map/reduce_scatter | solution.py:288
  9.0 1.5 %copy-start.6 = (s32[2,2,512]{2,1,0:T(2,128)S(1)}, s32[2,2,512]{2,1,0:T(2,128)}, u32[]{:S(2)}) copy-start(s32[2,2,512]{2,1,0:T(2,128)} %param.16) | copy-start | bytes 24580
  9.0 1.5 %copy-start.7 = (f32[128,8]{0,1:T(8,128)S(1)}, f32[128,8]{0,1:T(8,128)}, u32[]{:S(2)}) copy-start(f32[128,8]{0,1:T(8,128)} %param.17) | copy-start | bytes 12292
  10.9 0.7 copy-start.5
  10.9 0.7 copy-start.3
  11.0 0.7 copy-start.2
  11.7 0.7 copy-start.4
  12.4 0.7 copy-start.1
Sparse Core Ops, SparseCore 0:
  59.2 37.8 reduce-scatter.1
where the time goes:
time: 147 us
  blocking collectives  56.3 us (38%)
  waiting for transfers between devices  37.3 us (25%)
  Pallas kernels  31.7 us (22%)
  between operations  14.1 us (10%)
  local copies, waits for them, and re-layouts  6.89 us (5%)
    psum x1, blocking collectives, per_device(): sums = lax.psum(histogram(power_share, bins_share), ('freq', 'base'))  39.5 us
    reduce_scatter x1, waiting for transfers between devices, per_device(): lax.psum_scatter(power_part, 'freq', scatter_dimension=0, tiled=True)  37.3 us
    pallas_call x1, Pallas kernels, image_power(): pl.pallas_call(functools.partial(image_kernel, grid, scale), grid=(channe...  28.9 us
    all_gather x1, blocking collectives, per_device(): fields = lax.all_gather(fields, 'base', axis=2, tiled=True)  16.8 us
  transfers between devices with their start and end apart: 1, of which 1 were waited for; matrix products, arithmetic and copies ran while one was open for 0% of the time, Pallas kernels for 0%

commit v1 on v0

v1 whole, which is shorter than its diff:
```python
import functools
import math

import jax
import jax.numpy as jnp
import numpy as np
from jax import lax
from jax.experimental import pallas as pl
from jax.experimental.pallas import tpu as pltpu
from jax.sharding import PartitionSpec as P

NBINS = 512
BIN_LOW = 32
KW = 8
FINE = 32
SPREAD = FINE + KW
RADIX = 4
GROUP = 16
FIELDS = 8
LANES = 128
MESH = pl.DeviceIdType.MESH


def halves_of(x):
    high = x.astype(jnp.bfloat16)
    low = (x - high.astype(jnp.float32)).astype(jnp.bfloat16)
    return high, low


@functools.lru_cache(None)
def transform_tables(grid):
    slab = grid // RADIX
    u = RADIX * np.arange(slab)[None, None, :] + np.arange(RADIX)[:, None, None]
    angle = ((np.arange(slab)[None, :, None] * u) % grid) * (2.0 * math.pi / grid)
    x = np.concatenate([np.cos(angle), np.sin(angle)], axis=1).astype(np.float32)
    high = x.astype(jnp.bfloat16)
    low = (x - high.astype(np.float32)).astype(jnp.bfloat16)
    return high, low


def dot(a, b):
    return jnp.dot(a, b, preferred_element_type=jnp.float32)


def dot_rows(a, b):
    return lax.dot_general(a, b, (((1,), (1,)), ((), ())), preferred_element_type=jnp.float32)


def enter(peers):
    barrier = pltpu.get_barrier_semaphore()
    for peer in peers:
        pl.semaphore_signal(barrier, inc=1, device_id=peer, device_id_type=MESH)
    pl.semaphore_wait(barrier, len(peers))


def gather_kernel(
    split, base_count, tile_rows, grid, vis_ref, tile_ref, within_ref, column_ref, index_ref, live_ref,
    out_ref, send_sems, recv_sems
):
    freq, base = lax.axis_index("freq"), lax.axis_index("base")
    part = lax.rem(freq, split)
    first = freq - part
    channels, slots = within_ref.shape
    spot = pl.ds(pl.multiple_of(base * slots, slots), slots)
    lane = lax.broadcasted_iota(jnp.int32, (1, slots), 1)
    for c in range(channels):
        live = live_ref[c:c + 1, 0:1]
        is_live = lane < live
        u = jnp.minimum(tile_ref[c:c + 1, :] * tile_rows + within_ref[c:c + 1, :], grid - KW)
        rows = [
            jnp.where(is_live, vis_ref[0, c:c + 1, :], 0.0),
            jnp.where(is_live, vis_ref[1, c:c + 1, :], 0.0),
            u.astype(jnp.float32),
            column_ref[c:c + 1, :].astype(jnp.float32),
            index_ref[0, c:c + 1, :].astype(jnp.float32),
            index_ref[1, c:c + 1, :].astype(jnp.float32),
            jnp.broadcast_to(live, (1, slots)).astype(jnp.float32),
            jnp.zeros((1, slots), jnp.float32),
        ]
        out_ref[part * channels + c, :, spot] = jnp.concatenate(rows, axis=0)
    peers = []
    for d_part in range(split):
        for d_base in range(base_count):
            if d_part or d_base:
                peers.append({
                    "freq": first + lax.rem(part + d_part, split),
                    "base": lax.rem(base + d_base, base_count),
                })
    enter(peers)
    mine = out_ref.at[pl.ds(part * channels, channels), :, spot]
    copies = []
    for k, peer in enumerate(peers):
        copy = pltpu.make_async_remote_copy(
            src_ref=mine, dst_ref=mine, send_sem=send_sems.at[k], recv_sem=recv_sems.at[k],
            device_id=peer, device_id_type=MESH,
        )
        copy.start()
        copies.append(copy)
    for copy in copies:
        copy.wait()


def gather_fields(split, base_count, tile_rows, grid, *arrays):
    channels, slots = arrays[2].shape
    peers = split * base_count - 1
    vmem = pl.BlockSpec(memory_space=pltpu.VMEM)
    return pl.pallas_call(
        functools.partial(gather_kernel, split, base_count, tile_rows, grid),
        out_shape=jax.ShapeDtypeStruct((channels * split, FIELDS, slots * base_count), jnp.float32),
        in_specs=[vmem] * len(arrays),
        out_specs=vmem,
        scratch_shapes=[pltpu.SemaphoreType.DMA((peers,)), pltpu.SemaphoreType.DMA((peers,))],
        compiler_params=pltpu.CompilerParams(collective_id=0, has_side_effects=True),
    )(*arrays)


def phase(product, grid):
    half = grid // 2
    angle = ((product + half) & (grid - 1)) - half
    angle = angle.astype(jnp.float32) * (2.0 * math.pi / grid)
    return jnp.cos(angle), jnp.sin(angle)


def image_kernel(
    grid, scale, split, slots, f_ref, kernel_ref, dh_hbm, dl_hbm, out_ref,
    fine_ref, coarse_ref, h_ref, y_ref, dh_ref, dl_ref, sems
):
    channel = pl.program_id(0)
    cols = out_ref.shape[1]
    slab = grid // RADIX
    period = RADIX * GROUP
    coarse_count = grid // FINE
    piece = min(256, slots)
    load_h = pltpu.make_async_copy(dh_hbm, dh_ref, sems.at[0])
    load_l = pltpu.make_async_copy(dl_hbm, dl_ref, sems.at[1])

    @pl.when(channel == 0)
    def _():
        load_h.start()
        load_l.start()
        out_ref[...] = jnp.zeros_like(out_ref)
        left = (lax.axis_index("base") * split + lax.rem(lax.axis_index("freq"), split)) * cols
        l = left + lax.broadcasted_iota(jnp.int32, (cols, SPREAD), 0)
        c, s = phase(l * lax.broadcasted_iota(jnp.int32, (cols, SPREAD), 1), grid)
        fine = jnp.concatenate(
            [jnp.concatenate([c, s], axis=1), jnp.concatenate([-s, c], axis=1)], axis=0
        )
        fh, fl = halves_of(fine)
        fine_ref[...] = jnp.zeros_like(fine_ref)
        fine_ref[:, 0:2 * SPREAD] = fh
        fine_ref[:, 2 * SPREAD:4 * SPREAD] = fl
        fine_ref[:, 4 * SPREAD:6 * SPREAD] = fh
        l = left + lax.broadcasted_iota(jnp.int32, (cols, coarse_count), 0)
        c, s = phase(l * lax.broadcasted_iota(jnp.int32, (cols, coarse_count), 1) * FINE, grid)
        ch, cl = halves_of(jnp.concatenate([c, -s], axis=0))
        coarse_ref[:, 0:coarse_count] = ch
        coarse_ref[:, coarse_count:] = cl

    h_ref[...] = jnp.zeros_like(h_ref)
    taps_table = kernel_ref[...]

    def look_up(row):
        pieces = []
        for at in range(0, piece, LANES):
            index = jnp.broadcast_to(row[:, at:at + LANES], (KW, LANES))
            pieces.append(jnp.take_along_axis(taps_table, index, axis=1))
        return jnp.concatenate(pieces, axis=1)

    def piece_step(start):
        at = pl.ds(pl.multiple_of(start, piece), piece)
        re, im = f_ref[0, 0:1, at], f_ref[0, 1:2, at]
        u = f_ref[0, 2:3, at].astype(jnp.int32)
        v = f_ref[0, 3:4, at].astype(jnp.int32)
        taps_u = look_up(f_ref[0, 4:5, at].astype(jnp.int32))
        taps_v = look_up(f_ref[0, 5:6, at].astype(jnp.int32))

        offset = lax.broadcasted_iota(jnp.int32, (SPREAD, piece), 0) - (v & (FINE - 1))
        spread = jnp.zeros((SPREAD, piece), jnp.float32)
        for t in range(KW):
            spread = jnp.where(offset == t, taps_v[t:t + 1, :], spread)
        both = jnp.concatenate([spread * re, spread * im], axis=0)
        bh, bl = halves_of(both)
        pad = jnp.zeros((256 - 6 * SPREAD, piece), jnp.bfloat16)
        zb = dot(fine_ref[...], jnp.concatenate([bh, bh, bl, pad], axis=0))
        pick = lax.broadcasted_iota(jnp.int32, (2 * coarse_count, piece), 0) & (coarse_count - 1)
        onehot = jnp.where(pick == v // FINE, 1.0, 0.0).astype(jnp.bfloat16)
        e = dot(coarse_ref[...], onehot)
        zr, zi = zb[:cols], zb[cols:]
        er, ei = e[:cols], e[cols:]
        z = jnp.concatenate([zr * er - zi * ei, zr * ei + zi * er], axis=0)
        zh, zl = halves_of(z)

        for first in range(RADIX):
            residue = RADIX * lax.broadcasted_iota(jnp.int32, (GROUP, piece), 0) + first
            tap = (residue - u) & (period - 1)
            group = (u + tap - residue) // period
            r = jnp.zeros((GROUP, piece), jnp.float32)
            for t in range(KW):
                r = jnp.where(tap == t, taps_u[t:t + 1, :], r)
            rh, rl = halves_of(r)
            q = group.astype(jnp.float32).astype(jnp.bfloat16)
            zero = jnp.zeros_like(rh)
            hits = [q == jnp.bfloat16(g) for g in range(slab // GROUP)]
            wh = jnp.concatenate([jnp.where(hit, rh, zero) for hit in hits], axis=0)
            wl = jnp.concatenate([jnp.where(hit, rl, zero) for hit in hits], axis=0)
            h_ref[first] += dot_rows(wh, zh) + dot_rows(wh, zl) + dot_rows(wl, zh)

    blocks = f_ref.shape[2] // slots

    def block_step(block, carry):
        live = jnp.max(f_ref[0, 6:7, pl.ds(pl.multiple_of(block * slots, slots), LANES)])
        for inner in range(slots // piece):
            @pl.when(live > float(inner * piece))
            def _():
                piece_step(block * slots + inner * piece)
        return carry

    lax.fori_loop(0, blocks, block_step, 0)

    @pl.when(channel == 0)
    def _():
        load_h.wait()
        load_l.wait()

    def transform_step(first, carry):
        hh, hl = halves_of(h_ref[first])
        dh = dh_ref[first]
        y_ref[first] = dot(dh, hh) + dot(dh, hl) + dot(dl_ref[first], hh)
        return carry

    lax.fori_loop(0, RADIX, transform_step, 0)

    def combine(block, carry):
        rows = 32
        top = pl.multiple_of(block * rows, rows)
        low = pl.multiple_of(slab + block * rows, rows)
        yr, yi = [], []
        for first in range(RADIX):
            cy = y_ref[first, pl.ds(top, rows), :]
            sy = y_ref[first, pl.ds(low, rows), :]
            yr.append(cy[:, :cols] + sy[:, cols:])
            yi.append(cy[:, cols:] - sy[:, :cols])
        ar, ai = yr[0] + yr[2], yi[0] + yi[2]
        br, bi = yr[0] - yr[2], yi[0] - yi[2]
        cr, ci = yr[1] + yr[3], yi[1] + yi[3]
        dr, di = yr[1] - yr[3], yi[1] - yi[3]
        parts = [
            (ar + cr, ai + ci), (br + di, bi - dr), (ar - cr, ai - ci), (br - di, bi + dr)
        ]
        for k, (xr, xi) in enumerate(parts):
            at = pl.ds(pl.multiple_of(k * slab + block * rows, rows), rows)
            out_ref[at, :] += (xr * xr + xi * xi) * scale
        return carry

    lax.fori_loop(0, slab // 32, combine, 0)


def image_power(fields, taps_table, dh, dl, grid, cols, split, slots, scale):
    channels, field_count, total = fields.shape
    slab = grid // RADIX
    bf16, f32 = jnp.bfloat16, jnp.float32
    anywhere = pl.BlockSpec(memory_space=pl.ANY)
    return pl.pallas_call(
        functools.partial(image_kernel, grid, scale, split, slots),
        grid=(channels,),
        out_shape=jax.ShapeDtypeStruct((grid, cols), f32),
        in_specs=[
            pl.BlockSpec((1, field_count, total), lambda c: (c, 0, 0)),
            pl.BlockSpec(taps_table.shape, lambda c: (0, 0)),
            anywhere, anywhere,
        ],
        out_specs=pl.BlockSpec((grid, cols), lambda c: (0, 0)),
        scratch_shapes=[
            pltpu.VMEM((2 * cols, 256), bf16),
            pltpu.VMEM((2 * cols, 2 * (grid // FINE)), bf16),
            pltpu.VMEM((RADIX, slab, 2 * cols), f32),
            pltpu.VMEM((RADIX, 2 * slab, 2 * cols), f32),
            pltpu.VMEM(dh.shape, bf16),
            pltpu.VMEM(dl.shape, bf16),
            pltpu.SemaphoreType.DMA((2,)),
        ],
        compiler_params=pltpu.CompilerParams(
            vmem_limit_bytes=40 * 2**20, dimension_semantics=("arbitrary",)
        ),
    )(fields, taps_table, dh, dl)


def exchange_kernel(
    freq_count, base_count, split, power_ref, bins_ref, share_ref, spectrum_ref,
    recv_ref, a_ref, b_ref, stage_ref, stage2_ref, send_sems, recv_sems
):
    freq, base = lax.axis_index("freq"), lax.axis_index("base")
    share_rows, width = share_ref.shape
    cols = width // split
    ring = [{"freq": lax.rem(freq + d, freq_count), "base": base} for d in range(1, freq_count)]
    line = [{"freq": freq, "base": lax.rem(base + d, base_count)} for d in range(1, base_count)]
    enter(ring + line)
    copies = []
    for k, peer in enumerate(ring):
        top = pl.multiple_of(peer["freq"] * share_rows, share_rows)
        copy = pltpu.make_async_remote_copy(
            src_ref=power_ref.at[pl.ds(top, share_rows), :],
            dst_ref=recv_ref.at[freq],
            send_sem=send_sems.at[k], recv_sem=recv_sems.at[k],
            device_id=peer, device_id_type=MESH,
        )
        copy.start()
        copies.append(copy)
    recv_ref[freq] = power_ref[pl.ds(pl.multiple_of(freq * share_rows, share_rows), share_rows), :]
    bins = bins_ref[...].T
    for copy in copies:
        copy.wait()
    halves = []
    for part in range(split):
        total = recv_ref[part]
        for group in range(1, freq_count // split):
            total = total + recv_ref[group * split + part]
        halves.append(total)
    share_ref[...] = jnp.concatenate(halves, axis=1)

    rows, columns = share_rows, width
    high_count = NBINS // BIN_LOW
    for k in range(rows):
        at = slice(k * columns, (k + 1) * columns)
        value = share_ref[k:k + 1, :]
        bin_id = bins[k:k + 1, :]
        hit = lax.broadcasted_iota(jnp.int32, (high_count, columns), 0) == bin_id // BIN_LOW
        high = value.astype(jnp.bfloat16).astype(jnp.float32)
        low = value - high
        a_ref[0:high_count, at] = jnp.where(hit, high, 0.0).astype(jnp.bfloat16)
        a_ref[high_count:2 * high_count, at] = jnp.where(hit, low, 0.0).astype(jnp.bfloat16)
        a_ref[2 * high_count:, at] = jnp.where(hit, 1.0, 0.0).astype(jnp.bfloat16)
        hit = lax.broadcasted_iota(jnp.int32, (BIN_LOW, columns), 0) == bin_id % BIN_LOW
        b_ref[:, at] = jnp.where(hit, 1.0, 0.0).astype(jnp.bfloat16)
    sums = dot_rows(a_ref[...], b_ref[...])
    stage_ref[freq, 0] = sums[:high_count] + sums[high_count:2 * high_count]
    stage_ref[freq, 1] = sums[2 * high_count:]

    def share_out(ref, me, peers, offset):
        copies = []
        for k, peer in enumerate(peers):
            copy = pltpu.make_async_remote_copy(
                src_ref=ref.at[me], dst_ref=ref.at[me],
                send_sem=send_sems.at[offset + k], recv_sem=recv_sems.at[offset + k],
                device_id=peer, device_id_type=MESH,
            )
            copy.start()
            copies.append(copy)
        for copy in copies:
            copy.wait()
        total = ref[0]
        for other in range(1, ref.shape[0]):
            total = total + ref[other]
        return total

    stage2_ref[base] = share_out(stage_ref, freq, ring, len(ring))
    total = share_out(stage2_ref, base, line, 2 * len(ring))
    spectrum_ref[...] = total[0] / total[1]


def exchange(power, bins, freq_count, base_count, split, width):
    grid, cols = power.shape
    share_rows = grid // freq_count
    high_count = NBINS // BIN_LOW
    cells = share_rows * width
    sems = 2 * (freq_count - 1) + base_count - 1
    f32, bf16 = jnp.float32, jnp.bfloat16
    vmem = pl.BlockSpec(memory_space=pltpu.VMEM)
    return pl.pallas_call(
        functools.partial(exchange_kernel, freq_count, base_count, split),
        out_shape=(
            jax.ShapeDtypeStruct((share_rows, width), f32),
            jax.ShapeDtypeStruct((high_count, BIN_LOW), f32),
        ),
        in_specs=[vmem, vmem],
        out_specs=(vmem, vmem),
        scratch_shapes=[
            pltpu.VMEM((freq_count, share_rows, cols), f32),
            pltpu.VMEM((3 * high_count, cells), bf16),
            pltpu.VMEM((BIN_LOW, cells), bf16),
            pltpu.VMEM((freq_count, 2, high_count, BIN_LOW), f32),
            pltpu.VMEM((base_count, 2, high_count, BIN_LOW), f32),
            pltpu.SemaphoreType.DMA((sems,)),
            pltpu.SemaphoreType.DMA((sems,)),
        ],
        compiler_params=pltpu.CompilerParams(
            collective_id=1, has_side_effects=True, vmem_limit_bytes=40 * 2**20
        ),
    )(power, bins)


def per_device(visibility, tile_of, u_within, v_cell, kernel_index, kernel, live_count, bin_map):
    base_count = lax.axis_size("base")
    freq_count = lax.axis_size("freq")
    grid = bin_map.shape[1]
    width = grid // base_count
    split = 2 if width % (2 * LANES) == 0 and freq_count % 2 == 0 else 1
    channels_here, slots = u_within.shape
    dh, dl = transform_tables(grid)
    scale = 1.0 / (channels_here * freq_count * slots * base_count)
    fields = gather_fields(
        split, base_count, grid // base_count, grid,
        visibility, tile_of[:, :, 0], u_within, v_cell, kernel_index, live_count,
    )
    power = image_power(
        fields, kernel.T, jnp.asarray(dh), jnp.asarray(dl), grid, width // split, split, slots, scale
    )
    share_rows = grid // freq_count
    bins = lax.dynamic_slice_in_dim(bin_map, lax.axis_index("freq") * share_rows, share_rows, 1)
    share, spectrum = exchange(power, bins, freq_count, base_count, split, width)
    return share, spectrum.reshape(NBINS)


def solution(mesh):
    in_specs = (
        P(None, "freq", "base"),
        P("freq", "base", None),
        P("freq", "base"),
        P("freq", "base"),
        P(None, "freq", "base"),
        P(),
        P("freq", "base"),
        P("base", None),
    )
    out_specs = (P("freq", "base"), P())
    return jax.shard_map(
        per_device, mesh=mesh, in_specs=in_specs, out_specs=out_specs, check_vma=False
    )
```

time: 147 us -> 72.3 us (0.49)
  blocking collectives: 56.3 us -> 0 us
  waiting for transfers between devices: 37.3 us -> 0 us
  Pallas kernels: 31.7 us -> 64.5 us
  between operations: 14.1 us -> 0.7 us
    psum x1 -> x0, blocking collectives: 39.5 us -> none  [per_device(): sums = lax.psum(histogram(power_share, bins_share), ('freq', 'base'))]
    reduce_scatter x1 -> x0, waiting for transfers between devices: 37.3 us -> none  [per_device(): lax.psum_scatter(power_part, 'freq', scatter_dimension=0, tiled=True)]
    pallas_call x2 -> x3, Pallas kernels: 31.7 us -> 64.5 us  [the longest x1 28.8 us: image_power(): pl.pallas_call(functools.partial(image_kernel, grid, scale, split, slots)...]
    all_gather x1 -> x0, blocking collectives: 16.8 us -> none  [per_device(): fields = lax.all_gather(fields, 'base', axis=2, tiled=True)]
    unnamed x16 -> x15, local copies, waits for them, and re-layouts: 2.01 us -> 6.73 us
    squeeze x3 -> x0, local copies, waits for them, and re-layouts: 3.27 us -> none  [the longest x1 1.76 us: per_device(): fine = lax.dynamic_index_in_dim(jnp.asarray(fine), here, 0, keepdims=False)]
  transfers between devices with their start and end apart: 1 -> 0, of which waited for: 1 -> 0; matrix products, arithmetic and copies ran while one was open for 0% -> 0% of each run, Pallas kernels for 0% -> 0%
where the time goes in v1:
time: 72.3 us; the launch traced here: 72.6 us
  Pallas kernels  64.5 us (89%)
  local copies, waits for them, and re-layouts  7.41 us (10%)
    pallas_call x1, Pallas kernels, image_power(): pl.pallas_call(functools.partial(image_kernel, grid, scale, split, slots)...  28.8 us
    pallas_call x1, Pallas kernels, exchange(): pl.pallas_call(functools.partial(exchange_kernel, freq_count, base_count,...  22.6 us
    pallas_call x1, Pallas kernels, gather_fields(): pl.pallas_call(functools.partial(gather_kernel, split, base_count, tile_r...  13.1 us
    unnamed x15, local copies, waits for them, and re-layouts  6.73 us

profile of v1, /device:TPU:0, one launch (start us, length us, event | category | flops | bytes accessed | tf_op | source)
XLA Modules:
  0.0 72.6 jit_solution(4076531941044567550)
XLA Ops:
  0.6 0.0 copy-start
  0.6 1.4 %copy.15 = s32[2,512,1]{1,0,2:T(2,128)} copy(s32[2,512,1]{1,2,0:T(1,128)} %param.11) | data formatting | bytes 8192
  2.0 0.0 copy-start.5
  2.0 0.7 copy-done.5
  2.7 0.6 copy.12.live_ref
  3.3 0.0 copy-start.4
  3.3 13.1 %shard_map.113.f_ref = f32[4,8,2048]{2,1,0:T(8,128)} custom-call(f32[2,2,512]{2,1,0:T(2,128)} %vis_ref.1, s32[2,512]{1,0:T(2,128)} %bitcast.5, s32[2,512]{1,0:T(2,128)} %within_ref.1, s32[2,512]{1,0:T(2,128)} %column_ref.1, s32[2,2,512]{2,1,0:T(2,128)} %index_ref.1, s32[2,1]{1,0:T(2,128)} %copy.12.live_ref), custom_call_target="tpu_custom_call" | custom-call | tf_op jit(solution)/shard_map/pallas_call | solution.py:107
  16.4 0.0 copy-done.4
  16.4 0.0 copy-start.1
  16.4 1.2 %copy-done.1 = bf16[4,512,256]{2,1,0:T(8,128)(2,1)S(1)} copy-done((bf16[4,512,256]{2,1,0:T(8,128)(2,1)S(1)}, bf16[4,512,256]{2,1,0:T(8,128)(2,1)}, u32[]{:S(2)}) %copy-start.1) | copy-done | bytes 1048600
  17.6 0.0 copy-start.2
  17.6 1.2 %copy-done.2 = bf16[4,512,256]{2,1,0:T(8,128)(2,1)S(1)} copy-done((bf16[4,512,256]{2,1,0:T(8,128)(2,1)S(1)}, bf16[4,512,256]{2,1,0:T(8,128)(2,1)}, u32[]{:S(2)}) %copy-start.2) | copy-done | bytes 1048600
  18.9 0.0 copy-start.3
  18.9 0.9 %copy-done.3 = f32[4,8,2048]{2,1,0:T(8,128)S(1)} copy-done((f32[4,8,2048]{2,1,0:T(8,128)S(1)}, f32[4,8,2048]{2,1,0:T(8,128)}, u32[]{:S(2)}) %copy-start.3) | copy-done | bytes 262168
  19.8 28.8 %shard_map.114.power_ref = f32[1024,128]{1,0:T(8,128)S(1)} custom-call(f32[4,8,2048]{2,1,0:T(8,128)S(1)} %copy-done.3, f32[8,128]{1,0:T(8,128)S(1)} %bitcast.4, bf16[4,512,256]{2,1,0:T(8,128)(2,1)S(1)} %copy-done.1, bf16[4,512,256]{2,1,0:T(8,128)(2,1)S(1)} %copy-done.2), custom_call_target="tpu_custom_call" | custom-call | tf_op jit(solution)/shard_map/pallas_call | solution.py:263
  48.6 0.0 copy-done
  48.6 22.6 %shard_map.115 = (f32[128,256]{1,0:T(8,128)S(1)}, f32[16,32]{1,0:T(8,128)S(1)}) custom-call(f32[1024,128]{1,0:T(8,128)S(1)} %shard_map.114.power_ref, s32[256,128]{1,0:T(8,128)S(1)} %constant_dynamic-slice_fusion.bins_ref), custom_call_target="tpu_custom_call" | custom-call | tf_op jit(solution)/shard_map/pallas_call | solution.py:369
  71.3 0.7 reshape.7
  72.0 0.7 copy.17
  (1 shorter events, 0.0 us)
Async XLA Ops:
  0.6 48.0 %copy-start = (s32[256,1024]{1,0:T(8,128)S(1)}, s32[256,1024]{1,0:T(8,128)}, u32[]{:S(2)}) copy-start(s32[256,1024]{1,0:T(8,128)} %param.17) | copy-start | bytes 3145732
  2.0 0.7 copy-start.5
  3.3 13.1 %copy-start.4 = (f32[128,8]{0,1:T(8,128)S(1)}, f32[128,8]{0,1:T(8,128)}, u32[]{:S(2)}) copy-start(f32[128,8]{0,1:T(8,128)} %param.15) | copy-start | bytes 12292
  16.4 1.2 %copy-start.1 = (bf16[4,512,256]{2,1,0:T(8,128)(2,1)S(1)}, bf16[4,512,256]{2,1,0:T(8,128)(2,1)}, u32[]{:S(2)}) copy-start(bf16[4,512,256]{2,1,0:T(8,128)(2,1)} %constant.16.clone.dh_hbm) | copy-start | bytes 3145732
  17.6 1.2 %copy-start.2 = (bf16[4,512,256]{2,1,0:T(8,128)(2,1)S(1)}, bf16[4,512,256]{2,1,0:T(8,128)(2,1)}, u32[]{:S(2)}) copy-start(bf16[4,512,256]{2,1,0:T(8,128)(2,1)} %constant.17.clone.dl_hbm) | copy-start | bytes 3145732
  18.9 0.9 %copy-start.3 = (f32[4,8,2048]{2,1,0:T(8,128)S(1)}, f32[4,8,2048]{2,1,0:T(8,128)}, u32[]{:S(2)}) copy-start(f32[4,8,2048]{2,1,0:T(8,128)} %shard_map.113.f_ref) | copy-start | bytes 786436
